TPU v7x, 512 devices: a whole 4x8x8 slice. The times are simulated.
512 devices in a mesh: dp: 128 (over x, y, z_hi, core), tensor: 4 (over z_lo).
Axes of the slice: x: 4, y: 8, z: 8 (z_hi: 2, z_lo: 4; z = z_hi * 4 + z_lo), core: 2. Of those that a mesh axis runs over, the one named last changes fastest.
Arguments:
- inputs_x: bfloat16 [16384, 4096], P('dp', 'tensor'), may hold values from -6 to 6
- hidden: bfloat16 [16384, 14336], P('dp', 'tensor'), may hold values from -6 to 6
- grad_up: bfloat16 [16384, 14336], P('dp', 'tensor'), may hold values from -6 to 6
- grad_down: bfloat16 [16384, 4096], P('dp', 'tensor'), may hold values from -6 to 6
- proj_in_up: bfloat16 [4096, 64], P('tensor'), may hold values from -0.09375 to 0.09375
- proj_in_down: bfloat16 [14336, 64], P('tensor'), may hold values from -0.046875 to 0.046875
- proj_out_up: bfloat16 [14336, 64], P('tensor'), may hold values from -0.046875 to 0.046875
- proj_out_down: bfloat16 [4096, 64], P('tensor'), may hold values from -0.09375 to 0.09375
- lengths: int32 [256], P('dp'), may hold values from 16 to 64
- stored_grads: bfloat16 [3328, 8192], P('dp', 'tensor'), may hold values from -6 to 6
Outputs:
- gram: bfloat16 [8192, 128, 64], P('tensor', 'dp')
All inputs are finite; a program needn't handle non-finite values.
Results may differ from a plain program's by a relative error of at most 0.0034.
Values may be sent and summed in bfloat16 or wider, within the bound.
A program may use at most 64 MiB of HBM per device.

v0:
```python
import math

import jax
import jax.numpy as jnp
from jax import lax
from jax.sharding import PartitionSpec as P


def sent_to_all(shard, axis):
    length = lax.axis_size(axis)
    return lax.all_to_all(
        jnp.broadcast_to(shard[None], (length, *shard.shape)), axis, 0, 0, tiled=True
    )


def of_everyone(shard, axis):
    everything = sent_to_all(shard, axis)
    return jnp.sum(everything, axis=0)


def in_blocks(shard, dim, length):
    before, after = (shard.shape[:dim], shard.shape[dim + 1 :])
    return jnp.moveaxis(shard.reshape(*before, length, -1, *after), dim, 0)


def summed_on_arrival(shard, axis, dim):
    blocks = in_blocks(shard, dim, lax.axis_size(axis))
    arrived = lax.all_to_all(blocks, axis, split_axis=0, concat_axis=0, tiled=True)
    return arrived.sum(axis=0)


def side_by_side(arrays, axis, split_dim, concat_dim, along):
    widths = [a.shape[along] for a in arrays]
    both = jnp.concatenate(arrays, axis=along)
    filled = lax.all_to_all(both, axis, split_axis=split_dim, concat_axis=concat_dim, tiled=True)
    return tuple(jnp.split(filled, [sum(widths[:k]) for k in range(1, len(widths))], axis=along))


def laid_out(blocks, dim):
    blocks = jnp.moveaxis(blocks, 0, dim)
    dims = blocks.shape
    return blocks.reshape(*dims[:dim], dims[dim] * dims[dim + 1], *dims[dim + 2 :])


def gather_directly(shard, axis, dim):
    blocks = sent_to_all(shard, axis)
    return laid_out(blocks, dim)


def matmul(left, right):
    return jnp.dot(left, right, preferred_element_type=jnp.float32)


def pick_split(dp_count, sub_width, quarter, tensor_count):
    chosen = 1
    lowest = quarter // dp_count + quarter * tensor_count
    for bit in range(dp_count.bit_length()):
        factor = 1 << bit
        if dp_count % factor == 0 and sub_width % factor == 0:
            spent = quarter * factor // dp_count + quarter * tensor_count // factor
            if spent < lowest:
                lowest = spent
                chosen = factor
    return chosen


def local(
    inputs_x,
    hidden,
    grad_up,
    grad_down,
    proj_in_up,
    proj_in_down,
    proj_out_up,
    proj_out_down,
    lengths,
    stored_grads,
):
    examples = lengths.shape[0]
    slot_count = inputs_x.shape[0] // examples
    proj_width = proj_in_up.shape[1]
    tensor_count = lax.axis_size("tensor")
    out_share = proj_width // tensor_count
    layers = 2
    terms_in = jnp.stack([matmul(inputs_x, proj_in_up), matmul(hidden, proj_in_down)])
    terms_out = jnp.stack([matmul(grad_up, proj_out_up), matmul(grad_down, proj_out_down)])
    summed_in = of_everyone(terms_in, "tensor")
    summed_out = summed_on_arrival(terms_out, "tensor", 2)
    live_mask = (jnp.arange(slot_count, dtype=jnp.int32)[None, :] < lengths[:, None]).astype(
        jnp.float32
    )
    in_proj = summed_in.reshape(layers, examples, slot_count, proj_width).transpose(1, 2, 0, 3)
    out_proj = summed_out.reshape(layers, examples, slot_count, out_share).transpose(1, 2, 0, 3)
    out_proj = out_proj * live_mask[:, :, None, None]
    current = jnp.einsum("esla,eslb->ealb", out_proj, in_proj, precision=lax.Precision.HIGHEST)
    current = (current * (1.0 / math.sqrt(slot_count))).reshape(
        examples, out_share * layers * proj_width
    )
    local_rows = jnp.concatenate([current.astype(jnp.bfloat16), stored_grads], axis=0)
    row_count = local_rows.shape[0]
    quarter = local_rows.shape[1]
    dp_count = lax.axis_size("dp")
    sub_width = quarter // dp_count
    every_count = row_count * dp_count
    split = pick_split(dp_count, sub_width, quarter, tensor_count)
    row_blocks = dp_count // split
    tile_height = quarter // row_blocks
    narrow = sub_width // split
    row_pieces = local_rows.reshape(row_count, row_blocks, tile_height).transpose(1, 0, 2)
    row_pieces = jnp.broadcast_to(row_pieces[:, None], (row_blocks, split, row_count, tile_height))
    row_pieces = row_pieces.reshape(dp_count * row_count, tile_height)
    col_pieces = local_rows.reshape(row_count, dp_count, split, narrow).transpose(2, 0, 1, 3)
    col_pieces = col_pieces.reshape(split, row_count, dp_count * narrow)
    col_pieces = jnp.broadcast_to(
        col_pieces[None], (row_blocks, split, row_count, dp_count * narrow)
    )
    col_pieces = col_pieces.reshape(dp_count * row_count, dp_count * narrow)
    row_block, column_block = side_by_side((row_pieces, col_pieces), "dp", 0, 0, 1)
    columns = gather_directly(column_block, "tensor", 1)
    tile = lax.dot_general(
        row_block, columns, (((0,), (0,)), ((), ())), preferred_element_type=jnp.float32
    )
    tile = (tile * (1.0 / math.sqrt(every_count))).astype(jnp.bfloat16)
    tile = tile.reshape(tile_height, tensor_count, dp_count, narrow).transpose(2, 0, 1, 3)
    tile = tile.reshape(dp_count * tile_height, tensor_count * narrow)
    owned = lax.all_to_all(tile, "dp", split_axis=0, concat_axis=0, tiled=True)
    owned = owned.reshape(row_blocks, split, tile_height, tensor_count, narrow).transpose(
        0, 2, 3, 1, 4
    )
    return owned.reshape(quarter, 1, tensor_count * sub_width)


def solution(mesh):
    in_specs = (
        P("dp", "tensor"),
        P("dp", "tensor"),
        P("dp", "tensor"),
        P("dp", "tensor"),
        P("tensor", None),
        P("tensor", None),
        P("tensor", None),
        P("tensor", None),
        P("dp"),
        P("dp", "tensor"),
    )
    out_specs = P("tensor", "dp", None)
    return jax.shard_map(local, mesh=mesh, in_specs=in_specs, out_specs=out_specs, check_vma=False)
```

profile of v0, /device:TPU:1, one launch (start us, length us, event | category | flops | bytes accessed | tf_op | source)
XLA Modules:
  0.0 247.7 jit_solution(1282370009681346210)
XLA Ops:
  0.0 0.0 copy-start
  0.0 0.0 copy-start.3
  0.0 1.2 copy-done
  1.2 0.0 copy-start.2
  1.2 1.5 fusion.12
  2.7 1.2 fusion.13
  3.9 0.6 maximum_bitcast_fusion
  4.5 7.8 %all-to-all-start.1 = ((f32[4,2,128,16]{2,3,1,0:T(8,128)}), f32[4,2,128,16]{2,3,1,0:T(8,128)S(1)}, u32[]{:S(2)}, u32[]{:S(2)}) async-start(f32[4,2,128,16]{2,3,1,0:T(8,128)} %maximum_bitcast_fusion), calls=%async_computation.1 | async-start | bytes 131072 | tf_op jit(solution)/shard_map/all_to_all | solution.py:28
  12.3 1.2 convolution_bitcast_fusion.1
  13.5 1.7 convolution_bitcast_fusion
  15.2 1.7 all-to-all-done.1
  16.9 0.7 broadcast_in_dim.10
  17.6 3.4 %all-to-all-start = ((f32[4,2,128,64]{2,3,1,0:T(8,128)}), f32[4,2,128,64]{2,3,1,0:T(8,128)S(1)}, u32[]{:S(2)}, u32[]{:S(2)}) async-start(f32[4,2,128,64]{2,3,1,0:T(8,128)} %broadcast_in_dim.10), calls=%async_computation | async-start | bytes 524288 | tf_op jit(solution)/shard_map/all_to_all | solution.py:11
  21.0 0.0 copy-done.3
  21.0 0.1 compare_convert_fusion
  21.1 0.1 reshape.71
  21.2 5.4 %all-to-all-done = f32[4,2,128,64]{2,3,1,0:T(8,128)S(1)} async-done(((f32[4,2,128,64]{2,3,1,0:T(8,128)}), f32[4,2,128,64]{2,3,1,0:T(8,128)S(1)}, u32[]{:S(2)}, u32[]{:S(2)}) %all-to-all-start) | async-done | bytes 262176 | tf_op jit(solution)/shard_map/all_to_all | solution.py:11
  26.6 0.1 reshape.70
  26.8 0.3 fusion.9
  27.1 0.1 convert_element_type.22
  27.2 0.0 copy-done.2
  27.3 0.3 copy.40
  27.6 0.5 copy.41
  28.1 0.2 broadcast_in_dim.13
  28.3 0.3 broadcast_in_dim.11
  28.6 0.4 pad_maximum_fusion
  29.0 97.3 %all_to_all.33 = bf16[128,28,384]{2,1,0:T(8,128)(2,1)} all-to-all(bf16[128,28,384]{2,1,0:T(8,128)(2,1)S(1)} %pad_maximum_fusion), channel_id=1, replica_groups=mesh['dp'=128,'tensor'=4] {'dp'}, dimensions={0} | all-to-all | bytes 5505024 | tf_op jit(solution)/shard_map/all_to_all | solution.py:35
  126.3 5.2 %all_to_all.24 = bf16[3584,384]{1,0:T(8,128)(2,1)} reshape(bf16[128,28,384]{2,1,0:T(8,128)(2,1)} %all_to_all.33) | data formatting | bytes 5505024 | tf_op jit(solution)/shard_map/all_to_all | solution.py:35
  131.5 1.2 split.9
  132.8 0.5 copy.42
  133.3 0.3 broadcast_in_dim.14
  133.6 0.0 copy-start.1
  133.6 83.8 %all_to_all.34 = bf16[4,3584,128]{1,2,0:T(8,128)(2,1)S(1)} all-to-all(bf16[4,3584,128]{1,2,0:T(8,128)(2,1)S(1)} %broadcast_in_dim.14), channel_id=1, replica_groups=mesh['dp'=128,'tensor'=4] {'tensor'}, dimensions={0} | all-to-all | bytes 7340032 | tf_op jit(solution)/shard_map/all_to_all | solution.py:11
  217.4 0.0 copy-done.1
  217.4 1.2 fusion.5
  218.6 0.1 reshape.75
  218.7 0.2 copy.43
  218.9 27.8 %all_to_all.35 = bf16[128,256,4]{1,2,0:T(4,128)(2,1)S(1)} all-to-all(bf16[128,256,4]{1,2,0:T(4,128)(2,1)S(1)} %bitcast.60), channel_id=1, replica_groups=mesh['dp'=128,'tensor'=4] {'dp'}, dimensions={0} | all-to-all | bytes 524288 | tf_op jit(solution)/shard_map/all_to_all | solution.py:126
  246.8 0.1 copy.45
  246.9 0.8 reshape.77
  (10 shorter events, 0.2 us)
Async XLA Ops:
  0.0 1.2 copy-start
  0.0 21.0 %copy-start.3 = (s32[2]{0:T(128)S(1)}, s32[2]{0:T(128)}, u32[]{:S(2)}) copy-start(s32[2]{0:T(128)} %param.18) | copy-start | bytes 28
  1.2 26.0 %copy-start.2 = (bf16[26,2048]{1,0:T(8,128)(2,1)S(1)}, bf16[26,2048]{1,0:T(8,128)(2,1)}, u32[]{:S(2)}) copy-start(bf16[26,2048]{1,0:T(8,128)(2,1)} %param.19) | copy-start | bytes 319492
  4.5 12.4 %all-to-all-start.1 = ((f32[4,2,128,16]{2,3,1,0:T(8,128)}), f32[4,2,128,16]{2,3,1,0:T(8,128)S(1)}, u32[]{:S(2)}, u32[]{:S(2)}) async-start(f32[4,2,128,16]{2,3,1,0:T(8,128)} %maximum_bitcast_fusion), calls=%async_computation.1 | async-start | bytes 131072 | tf_op jit(solution)/shard_map/all_to_all | solution.py:28
  17.6 9.0 %all-to-all-start = ((f32[4,2,128,64]{2,3,1,0:T(8,128)}), f32[4,2,128,64]{2,3,1,0:T(8,128)S(1)}, u32[]{:S(2)}, u32[]{:S(2)}) async-start(f32[4,2,128,64]{2,3,1,0:T(8,128)} %broadcast_in_dim.10), calls=%async_computation | async-start | bytes 524288 | tf_op jit(solution)/shard_map/all_to_all | solution.py:11
  133.6 83.8 %copy-start.1 = (bf16[3584,384]{1,0:T(8,128)(2,1)S(1)}, bf16[3584,384]{1,0:T(8,128)(2,1)}, u32[]{:S(2)}) copy-start(bf16[3584,384]{1,0:T(8,128)(2,1)} %all_to_all.24) | copy-start | bytes 8257540
where the time goes:
time: 248 us
  blocking collectives  209 us (84%)
  local copies, waits for them, and re-layouts  12 us (5%)
  starting transfers between devices  11.2 us (5%)
  matrix products  7.08 us (3%)
  waiting for transfers between devices  7.05 us (3%)
    all_to_all x1, blocking collectives, side_by_side(): lax.all_to_all(both, axis, split_axis=split_dim, concat_axis=concat_dim,...  97.3 us
    all_to_all x1, blocking collectives, sent_to_all(): lax.all_to_all(jnp.broadcast_to(shard[None], (length, *shard.shape)), axi...  83.8 us
    all_to_all x1, blocking collectives, local(): owned = lax.all_to_all(tile, 'dp', split_axis=0, concat_axis=0, tiled=True)  27.8 us
    all_to_all x1, starting transfers between devices, summed_on_arrival(): lax.all_to_all(blocks, axis, split_axis=0, concat_axis=0, tiled=True)  7.8 us
    dot_general x4, matrix products, matmul(): return jnp.dot(left, right, preferred_element_type=jnp.float32)  5.56 us
    all_to_all x1, waiting for transfers between devices, sent_to_all(): lax.all_to_all(jnp.broadcast_to(shard[None], (length, *shard.shape)), axi...  5.39 us
    all_to_all x1, local copies, waits for them, and re-layouts, side_by_side(): lax.all_to_all(both, axis, split_axis=split_dim, concat_axis=concat_dim,...  5.21 us
  transfers between devices with their start and end apart: 2, of which 2 were waited for; matrix products, arithmetic and copies ran while one was open for 1% of the time, Pallas kernels for 0%

commit v1 on v0

v1 whole, which is shorter than its diff:
```python
import functools
import math

import jax
import jax.numpy as jnp
from jax import lax
from jax.experimental import pallas as pl
from jax.experimental.pallas import tpu as pltpu
from jax.sharding import PartitionSpec as P

MESH = pl.DeviceIdType.MESH
NX, NY, NH, NC, NT = 4, 8, 2, 2, 4


def matmul(left, right):
    return jnp.dot(left, right, preferred_element_type=jnp.float32)


def exchange(scale, lrow, rcol, out, la, rb, acc, cr, obuf,
             a1s, a1r, b1s, b1r, ts, tr, xs, xr, ys, yr, cs_s, cs_r, os_, or_, loc):
    d = lax.axis_index("dp")
    t = lax.axis_index("tensor")
    x, y, h, c = d // 32, (d // 4) % 8, (d // 2) % 2, d % 2
    slot = rcol.shape[1]

    def dev(dx=0, dy=0, dh=0, dc=0, dt=0):
        xx, yy, hh, cc = (x + dx) % NX, (y + dy) % NY, (h + dh) % NH, (c + dc) % NC
        return (((xx * NY + yy) * NH + hh) * NC + cc, (t + dt) % NT)

    def remote(src, dst, ss, rs, to):
        return pltpu.make_async_remote_copy(
            src_ref=src, dst_ref=dst, send_sem=ss, recv_sem=rs, device_id=to, device_id_type=MESH
        )

    barrier = pltpu.get_barrier_semaphore()
    partners = [dev(dx=i, dh=k) for i in range(1, NX) for k in range(NH)]
    partners += [dev(dy=i, dh=k) for i in range(NY) for k in range(NH) if i or k]
    partners += [dev(dt=k) for k in range(1, NT)] + [dev(dc=1)]
    for p in partners:
        pl.semaphore_signal(barrier, inc=1, device_id=p, device_id_type=MESH)
    pl.semaphore_wait(barrier, len(partners))

    sends = []

    def go(copy):
        copy.start()
        sends.append(copy)

    def lanes(k):
        return pl.ds(pl.multiple_of(((t - k) % NT) * 128, 128), 128)

    own_l = pltpu.make_async_copy(lrow.at[x], la.at[y, h, x], loc.at[0])
    own_l.start()
    own_r = pltpu.make_async_copy(rcol.at[y * 2 + h], rb.at[x, y * 2 + h, :, lanes(0)], loc.at[1])
    own_r.start()
    for k in range(NH):
        for i in range(NX):
            if i or k:
                go(remote(lrow.at[(x + i) % NX], la.at[y, h, x], a1s.at[i * 2 + k],
                          a1r.at[i * 2 + k], dev(dx=i, dh=k)))
        for i in range(NY):
            if i or k:
                go(remote(rcol.at[((y + i) % NY) * 2 + (h + k) % 2],
                          rb.at[x, y * 2 + h, :, lanes(0)], b1s.at[i * 2 + k],
                          b1r.at[i * 2 + k], dev(dy=i, dh=k)))

    def a1_wait(i, k):
        dst = la.at[y, (h + k) % 2, (x - i) % NX]
        remote(dst, dst, a1s.at[i * 2 + k], a1r.at[i * 2 + k], dev(dx=i, dh=k)).wait_recv()

    def b1_wait(i, k):
        dst = rb.at[x, ((y - i) % NY) * 2 + (h + k) % 2, :, lanes(0)]
        remote(dst, dst, b1s.at[i * 2 + k], b1r.at[i * 2 + k], dev(dy=i, dh=k)).wait_recv()

    def y_last(way, j):
        return 3 if way == j else 2

    def y_send(way, j, s):
        sign = 1 - 2 * way
        ref = la.at[(y - sign * s) % NY, (h + j) % 2]
        i = (way * 2 + j) * 4 + s
        go(remote(ref, ref, ys.at[i], yr.at[i], dev(dy=sign)))

    def y_wait(way, j, s):
        sign = 1 - 2 * way
        ref = la.at[(y - sign * (s + 1)) % NY, (h + j) % 2]
        i = (way * 2 + j) * 4 + s
        remote(ref, ref, ys.at[i], yr.at[i], dev(dy=sign)).wait_recv()

    def y_step(j, s):
        for way in range(2):
            if s <= y_last(way, j):
                y_wait(way, j, s)
                if s + 1 <= y_last(way, j):
                    y_send(way, j, s + 1)

    def x_piece(way, k, s, at):
        sign = 1 - 2 * way
        col = (x - sign * at) % NX
        if s == 0:
            return rb.at[col, :, :, lanes(k)]
        return rb.at[col, pl.ds(8 * way, 8), :, lanes(k)]

    def x_send(way, k, s):
        ref = x_piece(way, k, s, s)
        i = (way * 4 + k) * 2 + s
        go(remote(ref, ref, xs.at[i], xr.at[i], dev(dx=1 - 2 * way)))

    def x_wait(way, k, s):
        ref = x_piece(way, k, s, s + 1)
        i = (way * 4 + k) * 2 + s
        remote(ref, ref, xs.at[i], xr.at[i], dev(dx=1 - 2 * way)).wait_recv()

    def t_wait(k):
        ref = rb.at[x, :, :, lanes(k)]
        remote(ref, ref, ts.at[k], tr.at[k], dev(dt=k)).wait_recv()
        for way in range(2):
            x_send(way, k, 0)

    def x_forward(k):
        for way in range(2):
            x_wait(way, k, 0)
            x_send(way, k, 1)

    own_l.wait()
    for i in range(1, NX):
        a1_wait(i, 0)
    for way in range(2):
        y_send(way, 0, 0)
    own_r.wait()
    for k in range(NH):
        for i in range(NY):
            if i or k:
                b1_wait(i, k)
    for k in range(1, NT):
        ref = rb.at[x, :, :, lanes(0)]
        go(remote(ref, ref, ts.at[k], tr.at[k], dev(dt=k)))
    for way in range(2):
        x_send(way, 0, 0)
    for i in range(NX):
        a1_wait(i, 1)
    for way in range(2):
        y_send(way, 1, 0)
    y_step(0, 0)
    x_forward(0)
    t_wait(1)
    y_step(1, 0)
    t_wait(3)
    t_wait(2)
    y_step(0, 1)
    x_forward(1)
    y_step(1, 1)
    x_forward(3)
    y_step(0, 2)
    x_forward(2)
    y_step(1, 2)
    for k in (0, 1, 3, 2):
        for way in range(2):
            x_wait(way, k, 1)
    y_step(0, 3)
    y_step(1, 3)

    def one(i, _):
        left = rb[i].reshape(16 * slot, 512)
        right = la[:, :, i].reshape(16 * slot, 512)
        part = lax.dot_general(left, right, (((0,), (0,)), ((), ())),
                               preferred_element_type=jnp.float32)
        part = part.reshape(NT, NX, NC, 16, 512)

        @pl.when(i == 0)
        def _():
            acc[...] = part

        @pl.when(i > 0)
        def _():
            acc[...] += part

        return 0

    lax.fori_loop(0, NX, one, 0)
    swap = remote(acc.at[:, :, 1 - c], cr, cs_s.at[0], cs_r.at[0], dev(dc=1))
    swap.start()
    swap.wait_recv()
    for i in range(NX):
        obuf[i] = ((acc[:, i, c] + cr[:, i]) * scale).astype(jnp.bfloat16).reshape(64, 512)
    own_cols = pl.ds(pl.multiple_of(x * 512, 512), 512)
    for i in (2, 1, 3):
        go(remote(obuf.at[(x + i) % NX], out.at[:, own_cols], os_.at[i], or_.at[i], dev(dx=i)))
    own_o = pltpu.make_async_copy(obuf.at[x], out.at[:, own_cols], loc.at[2])
    own_o.start()
    for i in (1, 3, 2):
        from_cols = pl.ds(pl.multiple_of(((x - i) % NX) * 512, 512), 512)
        remote(obuf.at[i], out.at[:, from_cols], os_.at[i], or_.at[i], dev(dx=i)).wait_recv()
    own_o.wait()
    swap.wait_send()
    for copy in sends:
        copy.wait_send()


def of_everyone(shard, axis):
    length = lax.axis_size(axis)
    everything = lax.all_to_all(
        jnp.broadcast_to(shard[None], (length, *shard.shape)), axis, 0, 0, tiled=True
    )
    return jnp.sum(everything, axis=0)


def summed_on_arrival(shard, axis, dim):
    length = lax.axis_size(axis)
    before, after = (shard.shape[:dim], shard.shape[dim + 1 :])
    blocks = jnp.moveaxis(shard.reshape(*before, length, -1, *after), dim, 0)
    arrived = lax.all_to_all(blocks, axis, split_axis=0, concat_axis=0, tiled=True)
    return arrived.sum(axis=0)


def local(
    inputs_x,
    hidden,
    grad_up,
    grad_down,
    proj_in_up,
    proj_in_down,
    proj_out_up,
    proj_out_down,
    lengths,
    stored_grads,
):
    examples = lengths.shape[0]
    slot_count = inputs_x.shape[0] // examples
    proj_width = proj_in_up.shape[1]
    tensor_count = lax.axis_size("tensor")
    out_share = proj_width // tensor_count
    layers = 2
    terms_in = jnp.stack([matmul(inputs_x, proj_in_up), matmul(hidden, proj_in_down)])
    terms_out = jnp.stack([matmul(grad_up, proj_out_up), matmul(grad_down, proj_out_down)])
    summed_in = of_everyone(terms_in, "tensor")
    summed_out = summed_on_arrival(terms_out, "tensor", 2)
    live_mask = (jnp.arange(slot_count, dtype=jnp.int32)[None, :] < lengths[:, None]).astype(
        jnp.float32
    )
    in_proj = summed_in.reshape(layers, examples, slot_count, proj_width).transpose(1, 2, 0, 3)
    out_proj = summed_out.reshape(layers, examples, slot_count, out_share).transpose(1, 2, 0, 3)
    out_proj = out_proj * live_mask[:, :, None, None]
    current = jnp.einsum("esla,eslb->ealb", out_proj, in_proj, precision=lax.Precision.HIGHEST)
    current = (current * (1.0 / math.sqrt(slot_count))).reshape(
        examples, out_share * layers * proj_width
    )
    rows = jnp.concatenate([current.astype(jnp.bfloat16), stored_grads], axis=0)
    every_count = rows.shape[0] * lax.axis_size("dp")
    slot = 32
    rows = jnp.pad(rows, ((0, slot - rows.shape[0]), (0, 0)))
    lrow = rows.reshape(slot, NX, 512).transpose(1, 0, 2)
    rcol = rows.reshape(slot, NX, 16, 32).transpose(2, 0, 1, 3).reshape(16, slot, 128)
    vmem = pl.BlockSpec(memory_space=pltpu.VMEM)
    dma = pltpu.SemaphoreType.DMA
    owned = pl.pallas_call(
        functools.partial(exchange, 1.0 / math.sqrt(every_count)),
        out_shape=jax.ShapeDtypeStruct((64, 2048), jnp.bfloat16),
        in_specs=[vmem, vmem],
        out_specs=vmem,
        scratch_shapes=[
            pltpu.VMEM((NY, NH, NX, slot, 512), jnp.bfloat16),
            pltpu.VMEM((NX, NY * NH, slot, 512), jnp.bfloat16),
            pltpu.VMEM((NT, NX, NC, 16, 512), jnp.float32),
            pltpu.VMEM((NT, NX, 16, 512), jnp.float32),
            pltpu.VMEM((NX, 64, 512), jnp.bfloat16),
            dma((8,)), dma((8,)), dma((16,)), dma((16,)), dma((4,)), dma((4,)),
            dma((16,)), dma((16,)), dma((16,)), dma((16,)), dma((1,)), dma((1,)),
            dma((4,)), dma((4,)), dma((3,)),
        ],
        compiler_params=pltpu.CompilerParams(
            collective_id=0, has_side_effects=True, vmem_limit_bytes=40 * 1024 * 1024
        ),
        name="gram",
    )(lrow, rcol)
    return owned.T.reshape(2048, 1, 64)


def solution(mesh):
    in_specs = (
        P("dp", "tensor"),
        P("dp", "tensor"),
        P("dp", "tensor"),
        P("dp", "tensor"),
        P("tensor", None),
        P("tensor", None),
        P("tensor", None),
        P("tensor", None),
        P("dp"),
        P("dp", "tensor"),
    )
    out_specs = P("tensor", "dp", None)
    return jax.shard_map(local, mesh=mesh, in_specs=in_specs, out_specs=out_specs, check_vma=False)
```

time: 248 us -> 84.2 us (0.34)
  blocking collectives: 209 us -> 0 us
  Pallas kernels: 0 us -> 54.7 us
  local copies, waits for them, and re-layouts: 12 us -> 4.3 us
  matrix products: 7.08 us -> 2.63 us
    all_to_all x3 -> x0, blocking collectives: 209 us -> none  [the longest x1 97.3 us: side_by_side(): lax.all_to_all(both, axis, split_axis=split_dim, concat_axis=concat_dim,...]
    pallas_call x0 -> x1, Pallas kernels: none -> 54.7 us  [local(): pl.pallas_call(functools.partial(exchange, 1.0 / math.sqrt(every_count)),...]
    all_to_all x2 -> x0, local copies, waits for them, and re-layouts: 5.24 us -> none  [the longest x1 5.21 us: side_by_side(): lax.all_to_all(both, axis, split_axis=split_dim, concat_axis=concat_dim,...]
    dot_general x4, matrix products: 5.56 us -> 2.31 us  [matmul(): return jnp.dot(left, right, preferred_element_type=jnp.float32)]
where the time goes in v1:
time: 84.2 us; the launch traced here: 83.3 us
  Pallas kernels  54.7 us (65%)
  starting transfers between devices  11.3 us (13%)
  waiting for transfers between devices  9.3 us (11%)
  local copies, waits for them, and re-layouts  4.3 us (5%)
  matrix products  2.63 us (3%)
    pallas_call x1, Pallas kernels, local(): pl.pallas_call(functools.partial(exchange, 1.0 / math.sqrt(every_count)),...  54.7 us
    all_to_all x1, starting transfers between devices, summed_on_arrival(): lax.all_to_all(blocks, axis, split_axis=0, concat_axis=0, tiled=True)  7.8 us
    all_to_all x1, waiting for transfers between devices, of_everyone(): lax.all_to_all(jnp.broadcast_to(shard[None], (length, *shard.shape)), axi...  5.39 us
    all_to_all x1, waiting for transfers between devices, summed_on_arrival(): lax.all_to_all(blocks, axis, split_axis=0, concat_axis=0, tiled=True)  3.92 us
    all_to_all x1, starting transfers between devices, of_everyone(): lax.all_to_all(jnp.broadcast_to(shard[None], (length, *shard.shape)), axi...  3.54 us
    unnamed x19, local copies, waits for them, and re-layouts  2.35 us
    dot_general x4, matrix products, matmul(): return jnp.dot(left, right, preferred_element_type=jnp.float32)  2.31 us
  transfers between devices with their start and end apart: 2, of which 2 were waited for; matrix products, arithmetic and copies ran while one was open for 1% of the time, Pallas kernels for 0%

profile of v1, /device:TPU:1, one launch (start us, length us, event | category | flops | bytes accessed | tf_op | source)
XLA Modules:
  0.0 83.3 jit_solution(9012838442453047558)
XLA Ops:
  0.0 0.0 copy-start
  0.0 0.0 copy-start.5
  0.0 0.0 copy-start.3
  0.0 0.0 copy-start.1
  0.0 1.2 %copy-done = bf16[128,3584]{1,0:T(8,128)(2,1)S(1)} copy-done((bf16[128,3584]{1,0:T(8,128)(2,1)S(1)}, bf16[128,3584]{1,0:T(8,128)(2,1)}, u32[]{:S(2)}) %copy-start) | copy-done | bytes 917528
  1.2 0.0 copy-start.4
  1.2 0.0 copy-start.6
  1.2 1.5 %fusion.7 = f32[128,64]{0,1:T(8,128)S(1)} fusion(bf16[128,3584]{1,0:T(8,128)(2,1)S(1)} %copy-done, bf16[3584,64]{0,1:T(8,128)(2,1)} %param.16), kind=kOutput, calls=%fused_computation.17 | convolution fusion | flops 58720256 | bytes 1409024 | tf_op jit(solution)/shard_map/dot_general | solution.py:16
  2.7 0.0 copy-done.5
  2.7 0.0 copy-done.3
  2.7 0.0 copy-start.2
  2.7 0.2 fusion.8
  2.9 0.6 maximum_bitcast_fusion
  3.6 7.8 %all-to-all-start.1 = ((f32[4,2,128,16]{2,3,1,0:T(8,128)}), f32[4,2,128,16]{2,3,1,0:T(8,128)S(1)}, u32[]{:S(2)}, u32[]{:S(2)}) async-start(f32[4,2,128,16]{2,3,1,0:T(8,128)} %maximum_bitcast_fusion), calls=%async_computation.1 | async-start | bytes 131072 | tf_op jit(solution)/shard_map/all_to_all | solution.py:212
  11.4 0.0 copy-done.4
  11.4 0.0 copy-done.6
  11.4 0.2 convolution_bitcast_fusion.1
  11.6 0.0 copy-done.1
  11.6 0.0 copy-done.2
  11.6 0.4 convolution_bitcast_fusion
  12.0 3.9 %all-to-all-done.1 = f32[4,2,128,16]{2,3,1,0:T(8,128)S(1)} async-done(((f32[4,2,128,16]{2,3,1,0:T(8,128)}), f32[4,2,128,16]{2,3,1,0:T(8,128)S(1)}, u32[]{:S(2)}, u32[]{:S(2)}) %all-to-all-start.1) | async-done | bytes 65568 | tf_op jit(solution)/shard_map/all_to_all | solution.py:212
  15.9 0.7 broadcast_in_dim.2
  16.7 0.0 copy-start.8
  16.7 3.5 %all-to-all-start = ((f32[4,2,128,64]{2,3,1,0:T(8,128)}), f32[4,2,128,64]{2,3,1,0:T(8,128)S(1)}, u32[]{:S(2)}, u32[]{:S(2)}) async-start(f32[4,2,128,64]{2,3,1,0:T(8,128)} %broadcast_in_dim.2), calls=%async_computation | async-start | bytes 524288 | tf_op jit(solution)/shard_map/all_to_all | solution.py:202
  20.2 0.0 copy-done.8
  20.2 0.1 compare_convert_fusion
  20.3 0.1 reshape.49
  20.4 5.4 %all-to-all-done = f32[4,2,128,64]{2,3,1,0:T(8,128)S(1)} async-done(((f32[4,2,128,64]{2,3,1,0:T(8,128)}), f32[4,2,128,64]{2,3,1,0:T(8,128)S(1)}, u32[]{:S(2)}, u32[]{:S(2)}) %all-to-all-start) | async-done | bytes 262176 | tf_op jit(solution)/shard_map/all_to_all | solution.py:202
  25.8 0.1 reshape.48
  26.0 0.0 copy-start.7
  26.0 0.3 fusion.1
  26.3 0.1 convert_element_type.21
  26.4 0.5 copy-done.7
  26.9 0.4 reshape.51
  27.3 0.2 copy.33
  27.6 0.3 reshape.52.rcol
  27.9 54.7 %gram.1 = bf16[64,2048]{1,0:T(8,128)(2,1)S(1)} custom-call(bf16[4,32,512]{2,1,0:T(8,128)(2,1)S(1)} %bitcast.43, bf16[16,32,128]{2,1,0:T(8,128)(2,1)S(1)} %reshape.52.rcol), custom_call_target="tpu_custom_call" | custom-call | tf_op jit(solution)/shard_map/gram/pallas_call | solution.py:256
  82.6 0.7 copy.36
  (7 shorter events, 0.1 us)
Async XLA Ops:
  0.0 1.2 %copy-start = (bf16[128,3584]{1,0:T(8,128)(2,1)S(1)}, bf16[128,3584]{1,0:T(8,128)(2,1)}, u32[]{:S(2)}) copy-start(bf16[128,3584]{1,0:T(8,128)(2,1)} %param.12) | copy-start | bytes 2752516
  0.0 2.7 %copy-start.5 = (bf16[1024,64]{0,1:T(8,128)(2,1)S(1)}, bf16[1024,64]{0,1:T(8,128)(2,1)}, u32[]{:S(2)}) copy-start(bf16[1024,64]{0,1:T(8,128)(2,1)} %param.17) | copy-start | bytes 393220
  0.0 2.7 %copy-start.3 = (bf16[128,1024]{1,0:T(8,128)(2,1)S(1)}, bf16[128,1024]{1,0:T(8,128)(2,1)}, u32[]{:S(2)}) copy-start(bf16[128,1024]{1,0:T(8,128)(2,1)} %param.13) | copy-start | bytes 786436
  0.0 11.6 %copy-start.1 = (bf16[128,3584]{1,0:T(8,128)(2,1)S(1)}, bf16[128,3584]{1,0:T(8,128)(2,1)}, u32[]{:S(2)}) copy-start(bf16[128,3584]{1,0:T(8,128)(2,1)} %param.11) | copy-start | bytes 2752516
  1.2 10.2 %copy-start.4 = (bf16[128,1024]{1,0:T(8,128)(2,1)S(1)}, bf16[128,1024]{1,0:T(8,128)(2,1)}, u32[]{:S(2)}) copy-start(bf16[128,1024]{1,0:T(8,128)(2,1)} %param.10) | copy-start | bytes 786436
  1.2 10.2 %copy-start.6 = (bf16[1024,64]{0,1:T(8,128)(2,1)S(1)}, bf16[1024,64]{0,1:T(8,128)(2,1)}, u32[]{:S(2)}) copy-start(bf16[1024,64]{0,1:T(8,128)(2,1)} %param.14) | copy-start | bytes 393220
  2.7 8.9 %copy-start.2 = (bf16[3584,64]{0,1:T(8,128)(2,1)S(1)}, bf16[3584,64]{0,1:T(8,128)(2,1)}, u32[]{:S(2)}) copy-start(bf16[3584,64]{0,1:T(8,128)(2,1)} %param.15) | copy-start | bytes 1376260
  3.6 12.4 %all-to-all-start.1 = ((f32[4,2,128,16]{2,3,1,0:T(8,128)}), f32[4,2,128,16]{2,3,1,0:T(8,128)S(1)}, u32[]{:S(2)}, u32[]{:S(2)}) async-start(f32[4,2,128,16]{2,3,1,0:T(8,128)} %maximum_bitcast_fusion), calls=%async_computation.1 | async-start | bytes 131072 | tf_op jit(solution)/shard_map/all_to_all | solution.py:212
  16.7 3.6 %copy-start.8 = (s32[2]{0:T(128)S(1)}, s32[2]{0:T(128)}, u32[]{:S(2)}) copy-start(s32[2]{0:T(128)} %param.18) | copy-start | bytes 28
  16.7 9.1 %all-to-all-start = ((f32[4,2,128,64]{2,3,1,0:T(8,128)}), f32[4,2,128,64]{2,3,1,0:T(8,128)S(1)}, u32[]{:S(2)}, u32[]{:S(2)}) async-start(f32[4,2,128,64]{2,3,1,0:T(8,128)} %broadcast_in_dim.2), calls=%async_computation | async-start | bytes 524288 | tf_op jit(solution)/shard_map/all_to_all | solution.py:202
  26.0 0.9 %copy-start.7 = (bf16[26,2048]{1,0:T(8,128)(2,1)S(1)}, bf16[26,2048]{1,0:T(8,128)(2,1)}, u32[]{:S(2)}) copy-start(bf16[26,2048]{1,0:T(8,128)(2,1)} %param.19) | copy-start | bytes 319492

commit v2 on v0

v2 whole, which is shorter than its diff:
```python
import functools
import math

import jax
import jax.numpy as jnp
from jax import lax
from jax.experimental import pallas as pl
from jax.experimental.pallas import tpu as pltpu
from jax.sharding import PartitionSpec as P

MESH = pl.DeviceIdType.MESH
NX, NY, NH, NC, NT = 4, 8, 2, 2, 4
WAVES = 2
TILE = 16


def across(left, right):
    return lax.dot_general(
        left, right, (((1,), (1,)), ((), ())), preferred_element_type=jnp.float32
    )


def exchange(scale, own, slot_scale, new_at, lengths, lst, rst, ix, hid, gu, gd, piu, pid, pou, pod,
             out, la, rb, st, lcur, rcur, acc, cr, obuf, pin, rin, pout, rout,
             vix, vhid, vgu, vgd, vpiu, vpid, vpou, vpod,
             a1s, a1r, b1s, b1r, hls, hlr, hrs, hrr, ts, tr, xs, xr, ys, yr,
             ps, pr, qs, qr, cs, cr_sem, os_, or_, loc, load):
    d = lax.axis_index("dp")
    t = lax.axis_index("tensor")
    x, y, h, c = d // 32, (d // 4) % 8, (d // 2) % 2, d % 2

    def dev(dx=0, dy=0, dh=0, dc=0, dt=0):
        xx, yy, hh, cc = (x + dx) % NX, (y + dy) % NY, (h + dh) % NH, (c + dc) % NC
        return (((xx * NY + yy) * NH + hh) * NC + cc, (t + dt) % NT)

    def remote(src, dst, ss, rs, to):
        return pltpu.make_async_remote_copy(
            src_ref=src, dst_ref=dst, send_sem=ss, recv_sem=rs, device_id=to, device_id_type=MESH
        )

    barrier = pltpu.get_barrier_semaphore()
    partners = [dev(dh=1), dev(dc=1)]
    partners += [dev(dx=i) for i in range(1, NX)] + [dev(dy=i) for i in range(1, NY)]
    partners += [dev(dt=k) for k in range(1, NT)]
    for p in partners:
        pl.semaphore_signal(barrier, inc=1, device_id=p, device_id_type=MESH)

    pairs = ((gu, vgu), (pou, vpou), (gd, vgd), (pod, vpod),
             (hid, vhid), (pid, vpid), (ix, vix), (piu, vpiu))
    loads = [pltpu.make_async_copy(a, b, load.at[i]) for i, (a, b) in enumerate(pairs)]
    for copy in loads:
        copy.start()

    sends = []

    def go(copy):
        copy.start()
        sends.append(copy)

    def lanes(k):
        return pl.ds(pl.multiple_of(((t - k) % NT) * 128, 128), 128)

    def half(j):
        return (h + j) % NH

    def l_from(w):
        return lst.at[0] if w == 0 else lcur

    def r_from(w):
        return rst.at[0] if w == 0 else rcur

    def own_copies(w):
        l, r = l_from(w), r_from(w)
        return [
            pltpu.make_async_copy(l.at[x], la.at[w, y, h, x], loc.at[w * 3]),
            pltpu.make_async_copy(
                r.at[y, h], rb.at[w, x, y, h, :, lanes(0)], loc.at[w * 3 + 1]),
            pltpu.make_async_copy(r.at[y, 1 - h], st.at[w, y], loc.at[w * 3 + 2]),
        ]

    def a1(w, i, at):
        return remote(l_from(w).at[(x + i) % NX], la.at[w, y, h, (x - at) % NX],
                      a1s.at[w * 4 + i], a1r.at[w * 4 + i], dev(dx=i))

    def b1(w, j, i, at):
        n = (w * 2 + j) * 8 + i
        yy = (y - at) % NY
        dst = st.at[w, yy] if j else rb.at[w, x, yy, h, :, lanes(0)]
        return remote(r_from(w).at[(y + i) % NY, half(j)], dst, b1s.at[n], b1r.at[n], dev(dy=i))

    def start(w):
        mine = own_copies(w)
        for copy in mine:
            copy.start()
        for i in (2, 1, 3):
            go(a1(w, i, 0))
        for j in (1, 0):
            for i in (4, 3, 5, 2, 6, 1, 7):
                go(b1(w, j, i, 0))
        return mine

    def y_copy(w, way, j, s, at):
        sign = 1 - 2 * way
        ref = la.at[w, (y - sign * at) % NY, half(j)]
        n = ((w * 2 + way) * 2 + j) * 4 + s
        return remote(ref, ref, ys.at[n], yr.at[n], dev(dy=sign))

    def y_start(w, j):
        for way in range(2):
            go(y_copy(w, way, j, 0, 0))

    def y_step(w, j, s):
        for way in range(2):
            last = 3 if way == j else 2
            if s <= last:
                y_copy(w, way, j, s, s + 1).wait_recv()
                if s + 1 <= last:
                    go(y_copy(w, way, j, s + 1, s + 1))

    def x_copy(w, way, k, j, s, at):
        sign = 1 - 2 * way
        ref = rb.at[w, (x - sign * at) % NX, :, half(j), :, lanes(k)]
        n = (((w * 2 + way) * 4 + k) * 2 + j) * 2 + s
        return remote(ref, ref, xs.at[n], xr.at[n], dev(dx=sign))

    def x_start(w, k, j):
        for way in range(2):
            go(x_copy(w, way, k, j, 0, 0))

    def x_step(w, k, j):
        for way in range(2):
            x_copy(w, way, k, j, 0, 1).wait_recv()
            if way == j:
                go(x_copy(w, way, k, j, 1, 1))

    def x_end(w, k, j):
        x_copy(w, j, k, j, 1, 2).wait_recv()

    def t_copy(w, k, j, at):
        ref = rb.at[w, x, :, half(j), :, lanes(at)]
        n = (w * 4 + k) * 2 + j
        return remote(ref, ref, ts.at[n], tr.at[n], dev(dt=k))

    def t_start(w, j):
        for k in range(1, NT):
            go(t_copy(w, k, j, 0))
        x_start(w, 0, j)

    def t_step(w, k, j):
        t_copy(w, k, j, k).wait_recv()
        x_start(w, k, j)

    def hl(w, j):
        ref = la.at[w, y, half(j)]
        return remote(ref, ref, hls.at[w], hlr.at[w], dev(dh=1))

    def hr(w, j):
        return remote(st.at[w], rb.at[w, x, :, half(j), :, lanes(0)], hrs.at[w], hrr.at[w],
                      dev(dh=1))

    def s1(w, mine):
        mine[0].wait()
        for i in range(1, NX):
            a1(w, i, i).wait_recv()
        go(hl(w, 0))
        y_start(w, 0)

    def s2(w, mine):
        mine[2].wait()
        for i in range(1, NY):
            b1(w, 1, i, i).wait_recv()
        go(hr(w, 0))
        mine[1].wait()
        for i in range(1, NY):
            b1(w, 0, i, i).wait_recv()
        t_start(w, 0)

    def s3(w):
        hl(w, 1).wait_recv()
        y_start(w, 1)

    def s4(w):
        hr(w, 1).wait_recv()
        t_start(w, 1)

    for i in range(4):
        loads[i].wait()
    for l, (g, p) in enumerate(((vgu, vpou), (vgd, vpod))):
        pout[:, l] = across(p[...], g[...]).reshape(NT, 16, 128)
    for i in range(4, 8):
        loads[i].wait()
    pin[...] = jnp.concatenate(
        [across(vix[...], vpiu[...]), across(vhid[...], vpid[...])], axis=1)

    pl.semaphore_wait(barrier, len(partners))
    for k in range(1, NT):
        go(remote(pout.at[(t + k) % NT], rout.at[k], qs.at[k], qr.at[k], dev(dt=k)))
        go(remote(pin, rin.at[k], ps.at[k], pr.at[k], dev(dt=k)))
    first = start(0)

    def current():
        for k in range(1, NT):
            remote(pout.at[k], rout.at[k], qs.at[k], qr.at[k], dev(dt=k)).wait_recv()
            remote(pin, rin.at[k], ps.at[k], pr.at[k], dev(dt=k)).wait_recv()
        summed_in = pin[...] + rin[1] + rin[2] + rin[3]
        summed_out = pout[t] + rout[1] + rout[2] + rout[3]
        token = lax.broadcasted_iota(jnp.int32, (1, 1, 128), 2)
        masked = []
        for e in range(2):
            live = (token >= e * own) & (token < e * own + lengths[e])
            masked.append(jnp.where(live, summed_out, 0.0))
        left = jnp.concatenate(masked, axis=0).reshape(64, 128)
        product = lax.dot_general(
            left, summed_in, (((1,), (0,)), ((), ())),
            precision=lax.Precision.HIGHEST, preferred_element_type=jnp.float32,
        ) * slot_scale
        product = product.reshape(2, 2, 16, 128)
        lane = lax.broadcasted_iota(jnp.int32, (16, 128), 1)
        row = lax.broadcasted_iota(jnp.int32, (16, 128), 0)
        group = lane // 32
        kept = []
        for e in range(2):
            kept.append(jnp.where(lane < 64, product[e, 0], product[e, 1]))
        for a in range(16):
            block = lst[1, a // 4, :, (a % 4) * 128:(a % 4 + 1) * 128].astype(jnp.float32)
            for e in range(2):
                block = jnp.where(row == new_at + e, kept[e][a:a + 1, :], block)
            lcur[a // 4, :, (a % 4) * 128:(a % 4 + 1) * 128] = block.astype(jnp.bfloat16)
        moved = [[kept[e] if s == 0 else pltpu.roll(kept[e], 32 * s, 1) for s in range(4)]
                 for e in range(2)]
        for g in range(16):
            u, v = g // 4, g % 4
            block = rst[1, g // 2, g % 2].astype(jnp.float32)
            for e in range(2):
                picked = moved[e][(0 - v) % 4][u:u + 1, :]
                for b in range(1, 4):
                    picked = jnp.where(group[0:1] == b,
                                       moved[e][(b - v) % 4][4 * b + u:4 * b + u + 1, :], picked)
                block = jnp.where(row == new_at + e, picked, block)
            rcur[g // 2, g % 2] = block.astype(jnp.bfloat16)

    def contract(w):
        def one(i, _):
            left = rb[w, i].reshape(16 * TILE, 512)
            right = la[w, :, :, i].reshape(16 * TILE, 512)
            part = lax.dot_general(left, right, (((0,), (0,)), ((), ())),
                                   preferred_element_type=jnp.float32)
            acc[...] += part.reshape(NT, NX, NC, 16, 512)
            return 0

        lax.fori_loop(0, NX, one, 0)

    s1(0, first)
    s2(0, first)
    y_step(0, 0, 0)
    s3(0)
    s4(0)
    current()
    second = start(1)
    acc[...] = jnp.zeros_like(acc)

    def steps(w):
        yield lambda: (x_step(w, 0, 0), t_step(w, 1, 0), t_step(w, 3, 0), t_step(w, 2, 0))
        yield lambda: (y_step(w, 0, 1), y_step(w, 1, 0))
        yield lambda: (x_step(w, 0, 1), t_step(w, 1, 1), t_step(w, 3, 1), t_step(w, 2, 1))
        yield lambda: (y_step(w, 0, 2), y_step(w, 1, 1))
        yield lambda: (x_step(w, 1, 0), x_step(w, 3, 0), x_step(w, 2, 0))
        yield lambda: (y_step(w, 0, 3), y_step(w, 1, 2))
        yield lambda: (x_step(w, 1, 1), x_step(w, 3, 1), x_step(w, 2, 1))
        yield lambda: y_step(w, 1, 3)
        yield lambda: [x_end(w, k, j) for k in (0, 1, 3, 2) for j in range(2)]

    zero, late = list(steps(0)), list(steps(1))
    zero[0]()
    zero[1]()
    s1(1, second)
    zero[2]()
    s2(1, second)
    zero[3]()
    zero[4]()
    y_step(1, 0, 0)
    s3(1)
    s4(1)
    zero[5]()
    late[0]()
    zero[6]()
    late[1]()
    zero[7]()
    late[2]()
    zero[8]()
    late[3]()
    late[4]()
    contract(0)
    for step in late[5:]:
        step()
    contract(1)

    swap = remote(acc.at[:, :, 1 - c], cr, cs.at[0], cr_sem.at[0], dev(dc=1))
    swap.start()
    swap.wait_recv()
    for i in range(NX):
        obuf[i] = ((acc[:, i, c] + cr[:, i]) * scale).astype(jnp.bfloat16).reshape(64, 512)
    own_cols = pl.ds(pl.multiple_of(x * 512, 512), 512)
    for i in (2, 1, 3):
        go(remote(obuf.at[(x + i) % NX], out.at[:, own_cols], os_.at[i], or_.at[i], dev(dx=i)))
    own_o = pltpu.make_async_copy(obuf.at[x], out.at[:, own_cols], loc.at[6])
    own_o.start()
    for i in (1, 3, 2):
        from_cols = pl.ds(pl.multiple_of(((x - i) % NX) * 512, 512), 512)
        remote(obuf.at[i], out.at[:, from_cols], os_.at[i], or_.at[i], dev(dx=i)).wait_recv()
    own_o.wait()
    swap.wait_send()
    for copy in sends:
        copy.wait_send()


def local(
    inputs_x,
    hidden,
    grad_up,
    grad_down,
    proj_in_up,
    proj_in_down,
    proj_out_up,
    proj_out_down,
    lengths,
    stored_grads,
):
    examples = lengths.shape[0]
    slot_count = inputs_x.shape[0] // examples
    stored = stored_grads.shape[0]
    every_count = (stored + examples) * lax.axis_size("dp")
    rows = jnp.pad(stored_grads, ((0, WAVES * TILE - stored), (0, 0)))
    lst = rows.reshape(WAVES, TILE, NX, 512).transpose(0, 2, 1, 3)
    rst = rows.reshape(WAVES, TILE, NX, NY, NH, 32).transpose(0, 3, 4, 1, 2, 5)
    rst = rst.reshape(WAVES, NY, NH, TILE, 128)
    vmem = pl.BlockSpec(memory_space=pltpu.VMEM)
    smem = pl.BlockSpec(memory_space=pltpu.SMEM)
    hbm = pl.BlockSpec(memory_space=pltpu.HBM)
    dma = pltpu.SemaphoreType.DMA
    bf16, f32 = jnp.bfloat16, jnp.float32
    big = [inputs_x, hidden, grad_up, grad_down,
           proj_in_up.T, proj_in_down.T, proj_out_up.T, proj_out_down.T]
    owned = pl.pallas_call(
        functools.partial(exchange, 1.0 / math.sqrt(every_count), slot_count,
                          1.0 / math.sqrt(slot_count), stored - TILE),
        out_shape=jax.ShapeDtypeStruct((64, 2048), bf16),
        in_specs=[smem, vmem, vmem] + [hbm] * 8,
        out_specs=vmem,
        scratch_shapes=[
            pltpu.VMEM((WAVES, NY, NH, NX, TILE, 512), bf16),
            pltpu.VMEM((WAVES, NX, NY, NH, TILE, 512), bf16),
            pltpu.VMEM((WAVES, NY, TILE, 128), bf16),
            pltpu.VMEM((NX, TILE, 512), bf16),
            pltpu.VMEM((NY, NH, TILE, 128), bf16),
            pltpu.VMEM((NT, NX, NC, 16, 512), f32),
            pltpu.VMEM((NT, NX, 16, 512), f32),
            pltpu.VMEM((NX, 64, 512), bf16),
            pltpu.VMEM((128, 128), f32),
            pltpu.VMEM((NT, 128, 128), f32),
            pltpu.VMEM((NT, 2, 16, 128), f32),
            pltpu.VMEM((NT, 2, 16, 128), f32),
        ]
        + [pltpu.VMEM(a.shape, bf16) for a in big]
        + [dma((n,)) for n in (8, 8, 32, 32, 2, 2, 2, 2, 16, 16, 64, 64, 32, 32,
                               4, 4, 4, 4, 1, 1, 4, 4, 7, 8)],
        compiler_params=pltpu.CompilerParams(
            collective_id=0, has_side_effects=True, vmem_limit_bytes=40 * 1024 * 1024
        ),
        name="gram",
    )(lengths, lst, rst, *big)
    return owned.T.reshape(2048, 1, 64)


def solution(mesh):
    in_specs = (
        P("dp", "tensor"),
        P("dp", "tensor"),
        P("dp", "tensor"),
        P("dp", "tensor"),
        P("tensor", None),
        P("tensor", None),
        P("tensor", None),
        P("tensor", None),
        P("dp"),
        P("dp", "tensor"),
    )
    out_specs = P("tensor", "dp", None)
    return jax.shard_map(local, mesh=mesh, in_specs=in_specs, out_specs=out_specs, check_vma=False)
```

time: 248 us -> 74 us (0.30)
  blocking collectives: 209 us -> 0 us
  Pallas kernels: 0 us -> 66.1 us
  starting transfers between devices: 11.2 us -> 0 us
  matrix products: 7.08 us -> 0 us
  waiting for transfers between devices: 7.05 us -> 0 us
  local copies, waits for them, and re-layouts: 12 us -> 6.55 us
    all_to_all x3 -> x0, blocking collectives: 209 us -> none  [the longest x1 97.3 us: side_by_side(): lax.all_to_all(both, axis, split_axis=split_dim, concat_axis=concat_dim,...]
    pallas_call x0 -> x1, Pallas kernels: none -> 66.1 us  [local(): pl.pallas_call(functools.partial(exchange, 1.0 / math.sqrt(every_count),...]
    all_to_all x2 -> x0, starting transfers between devices: 11.2 us -> none  [the longest x1 7.8 us: summed_on_arrival(): lax.all_to_all(blocks, axis, split_axis=0, concat_axis=0, tiled=True)]
    dot_general x6 -> x0, matrix products: 7.08 us -> none  [the longest x4 5.56 us: matmul(): return jnp.dot(left, right, preferred_element_type=jnp.float32)]
    all_to_all x2 -> x0, waiting for transfers between devices: 7.05 us -> none  [the longest x1 5.39 us: sent_to_all(): lax.all_to_all(jnp.broadcast_to(shard[None], (length, *shard.shape)), axi...]
    all_to_all x2 -> x0, local copies, waits for them, and re-layouts: 5.24 us -> none  [the longest x1 5.21 us: side_by_side(): lax.all_to_all(both, axis, split_axis=split_dim, concat_axis=concat_dim,...]
  transfers between devices with their start and end apart: 2 -> 0, of which waited for: 2 -> 0; matrix products, arithmetic and copies ran while one was open for 1% -> 0% of each run, Pallas kernels for 0% -> 0%
where the time goes in v2:
time: 74 us; the launch traced here: 72.8 us
  Pallas kernels  66.1 us (89%)
  local copies, waits for them, and re-layouts  6.55 us (9%)
    pallas_call x1, Pallas kernels, local(): pl.pallas_call(functools.partial(exchange, 1.0 / math.sqrt(every_count),...  66.1 us
    unnamed x19, local copies, waits for them, and re-layouts  2.59 us

profile of v2, /device:TPU:1, one launch (start us, length us, event | category | flops | bytes accessed | tf_op | source)
XLA Modules:
  0.0 72.8 jit_solution(10321896998055894640)
XLA Ops:
  0.0 0.0 copy-start.4
  0.0 1.0 %pad.4 = bf16[32,2048]{1,0:T(8,128)(2,1)S(1)} pad(bf16[26,2048]{1,0:T(8,128)(2,1)} %param.19, bf16[]{:T(256)} %constant.2.clone.1), padding=0_6x0_0 | pad | bytes 237570 | tf_op jit(solution)/shard_map/jit(_pad)/pad | solution.py:333
  1.0 0.0 copy-start.3
  1.0 0.1 reshape.12
  1.1 0.0 copy-start.6
  1.1 0.0 copy-start.1
  1.1 0.4 reshape.13
  1.5 0.0 copy-start
  1.5 1.1 %copy.16 = bf16[2,16,4,8,2,32]{5,2,1,4,3,0:T(4,128)(2,1)} copy(bf16[2,16,4,8,2,32]{5,4,3,2,1,0:T(2,128)(2,1)S(1)} %reshape.13) | data formatting | bytes 262144 | tf_op jit(solution)/shard_map/reshape | solution.py:335
  2.6 0.0 copy-start.2
  2.6 0.0 copy-start.8
  2.6 1.4 %reshape.14.rst = bf16[2,8,2,16,128]{4,3,2,1,0:T(8,128)(2,1)S(1)} reshape(bf16[2,8,2,16,4,32]{5,4,3,2,1,0:T(4,128)(2,1)} %bitcast.19) | data formatting | bytes 262144 | tf_op jit(solution)/shard_map/reshape | solution.py:336
  4.0 0.0 copy-done.4
  4.1 0.0 copy-done.3
  4.1 0.0 copy-done.6
  4.1 0.0 copy-done.1
  4.1 0.0 copy-done
  4.1 0.0 copy-done.2
  4.1 0.0 copy-done.8
  4.1 0.0 copy-start.5
  4.1 0.9 %copy-done.5 = bf16[128,1024]{1,0:T(8,128)(2,1)S(1)} copy-done((bf16[128,1024]{1,0:T(8,128)(2,1)S(1)}, bf16[128,1024]{1,0:T(8,128)(2,1)}, u32[]{:S(2)}) %copy-start.5) | copy-done | bytes 262168
  5.1 0.0 copy-start.7
  5.1 0.9 %copy-done.7 = bf16[1024,64]{0,1:T(8,128)(2,1)S(1)} copy-done((bf16[1024,64]{0,1:T(8,128)(2,1)S(1)}, bf16[1024,64]{0,1:T(8,128)(2,1)}, u32[]{:S(2)}) %copy-start.7) | copy-done | bytes 131096
  6.0 66.1 %gram.1 = bf16[64,2048]{1,0:T(8,128)(2,1)S(1)} custom-call(s32[2]{0:T(128)S(1)} %copy-done.8, bf16[2,4,16,512]{3,2,1,0:T(8,128)(2,1)S(1)} %bitcast.14, bf16[2,8,2,16,128]{4,3,2,1,0:T(8,128)(2,1)S(1)} %reshape.14.rst, bf16[128,1024]{1,0:T(8,128)(2,1)S(1)} %copy-done.4, bf16[128,3584]{1,0:T(8,128)(2,1)S(1)} %copy-done, bf16[128,3584]{1,0:T(8,128)(2,1)S(1)} %copy-done.1, ...), custom_call_target="tpu_custom_call" | custom-call | tf_op jit(solution)/shard_map/gram/pallas_call | solution.py:344
  72.1 0.7 copy.19
  (1 shorter events, 0.0 us)
Async XLA Ops:
  0.0 4.0 %copy-start.4 = (bf16[128,1024]{1,0:T(8,128)(2,1)S(1)}, bf16[128,1024]{1,0:T(8,128)(2,1)}, u32[]{:S(2)}) copy-start(bf16[128,1024]{1,0:T(8,128)(2,1)} %ix.1) | copy-start | bytes 786436
  1.0 3.1 %copy-start.3 = (bf16[3584,64]{0,1:T(8,128)(2,1)S(1)}, bf16[3584,64]{0,1:T(8,128)(2,1)}, u32[]{:S(2)}) copy-start(bf16[3584,64]{0,1:T(8,128)(2,1)} %param.16) | copy-start | bytes 1376260
  1.1 3.0 %copy-start.6 = (bf16[1024,64]{0,1:T(8,128)(2,1)S(1)}, bf16[1024,64]{0,1:T(8,128)(2,1)}, u32[]{:S(2)}) copy-start(bf16[1024,64]{0,1:T(8,128)(2,1)} %param.14) | copy-start | bytes 393220
  1.1 3.0 %copy-start.1 = (bf16[128,3584]{1,0:T(8,128)(2,1)S(1)}, bf16[128,3584]{1,0:T(8,128)(2,1)}, u32[]{:S(2)}) copy-start(bf16[128,3584]{1,0:T(8,128)(2,1)} %gu.1) | copy-start | bytes 2752516
  1.5 2.6 %copy-start = (bf16[128,3584]{1,0:T(8,128)(2,1)S(1)}, bf16[128,3584]{1,0:T(8,128)(2,1)}, u32[]{:S(2)}) copy-start(bf16[128,3584]{1,0:T(8,128)(2,1)} %hid.1) | copy-start | bytes 2752516
  2.6 1.5 %copy-start.2 = (bf16[3584,64]{0,1:T(8,128)(2,1)S(1)}, bf16[3584,64]{0,1:T(8,128)(2,1)}, u32[]{:S(2)}) copy-start(bf16[3584,64]{0,1:T(8,128)(2,1)} %param.15) | copy-start | bytes 1376260
  2.6 1.5 %copy-start.8 = (s32[2]{0:T(128)S(1)}, s32[2]{0:T(128)}, u32[]{:S(2)}) copy-start(s32[2]{0:T(128)} %lengths.1) | copy-start | bytes 28
  4.1 1.0 %copy-start.5 = (bf16[128,1024]{1,0:T(8,128)(2,1)S(1)}, bf16[128,1024]{1,0:T(8,128)(2,1)}, u32[]{:S(2)}) copy-start(bf16[128,1024]{1,0:T(8,128)(2,1)} %gd.1) | copy-start | bytes 786436
  5.1 0.9 %copy-start.7 = (bf16[1024,64]{0,1:T(8,128)(2,1)S(1)}, bf16[1024,64]{0,1:T(8,128)(2,1)}, u32[]{:S(2)}) copy-start(bf16[1024,64]{0,1:T(8,128)(2,1)} %param.17) | copy-start | bytes 393220
